TPU v7x, 32 devices: a whole 2x2x4 slice. The times are simulated.
32 devices in a mesh: traj: 16 (over z, y, core), tm: 2 (over x).
Axes of the slice: x: 2, y: 2, z: 4, core: 2. Of those that a mesh axis runs over, the one named last changes fastest.
Arguments:
- states: float32 [2, 32, 4096], P('tm', None, 'traj'), may hold values from -6 to 6
- vectors: bfloat16 [64, 4096], P(None, 'traj'), may hold values from -6 to 6
- kernel_scale: float32 [2], P('tm'), may hold values from 6 to 16
- neighbour_blocks: int32 [32, 24], P('traj'), may hold values from 0 to 31, as said below
- neighbour_count: int32 [32], P('traj'), may hold values from 6 to 24, as said below
Outputs:
- result: float32 [64, 4096], P(None, 'traj')
Inputs may be any that keep to these rules, and one draw needn't show every extreme that they name: `neighbour_blocks`: row b names 24 different blocks, the first of them b itself. Only the first neighbour_count[b] entries of row b of neighbour_blocks are neighbours of block b; some block uses all 24.
All inputs are finite; a program needn't handle non-finite values.
Results may differ from a plain program's by a relative error of at most 0.0013.
Values may be sent and summed in bfloat16 or wider, within the bound.
No kernel may reach another device: no remote copies, remote signals or barrier semaphores. Data moves between devices by JAX's collectives and lax.ppermute only.
A program may use at most 64 MiB of HBM per device.

v0:
```python
import functools
import math

import jax
import jax.numpy as jnp
from jax import lax
from jax.experimental import pallas as pl
from jax.experimental.pallas import tpu as pltpu
from jax.sharding import PartitionSpec as P


BLK = 128
AUX = 8
LINK_ROW = 6
LIST_ROW = 7
GROUP = 2
COVER = 10000000
BIG = 52
SMALL = 16
ROUND = 27


VMEM = pl.BlockSpec(memory_space=pltpu.VMEM)
SMEM = pl.BlockSpec(memory_space=pltpu.SMEM)
HBM = pl.BlockSpec(memory_space=pltpu.HBM)
PARAMS = pltpu.CompilerParams(vmem_limit_bytes=16 * 1024 * 1024)


def plan(n):
    core = 2 if n % 2 == 0 else 1
    wide = 4 if n % (4 * core) == 0 else 1
    mid = n // (core * wide)
    stride = core * mid
    steps = []

    def middle(piece):
        return [(piece, k * core) for k in range(1, mid)]

    if wide == 4:
        steps += [(0, 2 * stride), (0, stride)] + middle(0) + [(2 * stride, stride)]
        steps += middle(2 * stride) + middle(stride) + middle(3 * stride)
    else:
        steps += middle(0)
    order = [0] + [piece ^ hop for piece, hop in steps]
    if core == 2:
        steps += [(piece, 1) for piece in order]
    return steps


def staged_gather(x, n, axis, tied):
    pieces = {0: x}
    for i, (piece, hop) in enumerate(plan(n)):
        if i == 1:
            pieces[0], tied = lax.optimization_barrier((pieces[0], tied))
        pieces[piece ^ hop] = lax.ppermute(pieces[piece], axis, [(d, d ^ hop) for d in range(n)])
    return [pieces[o] for o in range(n)], tied


def split3(value):
    first = value.astype(jnp.bfloat16)
    rest = value - first.astype(jnp.float32)
    second = rest.astype(jnp.bfloat16)
    third = (rest - second.astype(jnp.float32)).astype(jnp.bfloat16)
    return [p.astype(jnp.float32) for p in (first, second, third)]


def prep_kernel(blocks, lists_hbm, count_hbm, states_hbm, vectors_hbm, msg_ref, lists_ref, count_ref, states_ref, sems):
    vecs = vectors_hbm.shape[0]
    coords, rows = states_ref.shape[1], states_ref.shape[2]
    moves = [
        pltpu.make_async_copy(lists_hbm, lists_ref, sems.at[0]),
        pltpu.make_async_copy(count_hbm, count_ref, sems.at[1]),
        pltpu.make_async_copy(states_hbm, states_ref, sems.at[2]),
        pltpu.make_async_copy(vectors_hbm, msg_ref.at[0:vecs, :], sems.at[3]),
    ]
    for move in moves:
        move.start()
    for move in moves:
        move.wait()
    x = states_ref[0]
    hi = x.astype(jnp.bfloat16).astype(jnp.float32)
    lo = (x - hi).astype(jnp.bfloat16).astype(jnp.float32)
    whole = hi + lo
    pieces = split3(-0.5 * jnp.sum(whole * whole, axis=0, keepdims=True))
    lane = lax.broadcasted_iota(jnp.int32, (1, rows), 1)
    linked = jnp.zeros((1, rows), jnp.float32)
    listed = jnp.full((1, rows), blocks, jnp.int32)
    for h in range(rows // BLK):
        for slot in range(lists_ref.shape[1]):
            used = slot < count_ref[h]
            linked = jnp.where(lane == jnp.where(used, lists_ref[h, slot] + h * BLK, rows), 1.0, linked)
            listed = jnp.where(lane == slot + h * BLK, jnp.where(used, lists_ref[h, slot], blocks), listed)
        units = lax.shift_right_logical(count_ref[h] + (GROUP - 1), GROUP.bit_length() - 1)
        listed = jnp.where(lane == (h + 1) * BLK - 1, units, listed)
    sub = lax.broadcasted_iota(jnp.int32, (AUX, rows), 0)
    aux = jnp.where((sub >= 3) & (sub < 6), 1.0, 0.0)
    for r, piece in enumerate(pieces):
        aux = jnp.where(sub == r, piece, aux)
    aux = jnp.where(sub == LINK_ROW, linked, aux)
    aux = jnp.where(sub == LIST_ROW, listed.astype(jnp.float32), aux)
    msg_ref[vecs : vecs + coords, :] = hi.astype(jnp.bfloat16)
    msg_ref[vecs + coords : vecs + 2 * coords, :] = lo.astype(jnp.bfloat16)
    msg_ref[vecs + 2 * coords :, :] = aux.astype(jnp.bfloat16)


def factor_kernel(scale_ref, out_ref):
    out_ref[...] = (2.0 * math.log2(math.e)) / jnp.full(out_ref.shape, scale_ref[0], jnp.float32)


def right_side(msg, vecs, cols):
    feats = msg[vecs : msg.shape[0] - AUX, cols]
    return jnp.concatenate([feats, feats, msg[msg.shape[0] - AUX :, cols]], axis=0)


def stage_block(msg, vecs, base, right_ref, vec_ref):
    for h in range(msg.shape[1] // BLK):
        cols = slice(h * BLK, (h + 1) * BLK)
        right_ref[base + h] = right_side(msg, vecs, cols)
        vec_ref[base + h] = msg[0:vecs, cols]


def left_kernel(half, vecs, me_ref, *refs):
    msgs, (left_ref, lists_ref, right_ref, vec_ref, sums_ref, pushed_ref) = refs[:half], refs[half:]
    rows = msgs[0].shape[1]
    per = rows // BLK
    coords = (msgs[0].shape[0] - vecs - AUX) // 2
    blocks = 2 * half * per
    me = me_ref[0]
    sub = lax.broadcasted_iota(jnp.int32, (AUX, rows), 0)
    for m in range(half):
        hi = msgs[m][vecs : vecs + coords, :].astype(jnp.float32)
        lo = msgs[m][vecs + coords : vecs + 2 * coords, :].astype(jnp.float32)
        aux = msgs[m][vecs + 2 * coords :, :].astype(jnp.float32)
        left = jnp.where(sub < 3, 1.0, jnp.where(sub < 6, pltpu.roll(aux, 3, 0), 0.0))
        stacked = jnp.concatenate([hi, hi, lo, lo, left], axis=0).T.astype(jnp.bfloat16)
        for h in range(per):
            left_ref[m * per + h] = stacked[h * BLK : (h + 1) * BLK, :]
            row = aux[LIST_ROW : LIST_ROW + 1, h * BLK : (h + 1) * BLK]
            lists_ref[m * per + h : m * per + h + 1, :] = row.astype(jnp.int32)
        stage_block(msgs[m], vecs, (me ^ (2 * m)) * per, right_ref, vec_ref)
    lists_ref[half * per :, :] = jnp.zeros((8, BLK), jnp.int32)
    left_ref[half * per] = jnp.zeros(left_ref.shape[1:], jnp.bfloat16)
    sub = lax.broadcasted_iota(jnp.int32, right_ref.shape[1:], 0)
    right_ref[blocks] = jnp.where(sub == 4 * coords, -3.0e4, 0.0).astype(jnp.bfloat16)
    vec_ref[blocks] = jnp.zeros(vec_ref.shape[1:], jnp.bfloat16)
    sums_ref[...] = jnp.zeros(sums_ref.shape, jnp.float32)
    pushed_ref[...] = jnp.zeros(pushed_ref.shape, jnp.float32)


def push_kernel(half, vecs, most, me_ref, factor_ref, lists_ref, left_ref, *refs):
    msgs, refs = refs[:half], refs[half + 4 :]
    right_ref, vec_ref, sums_ref, pushed_ref, scaled_ref, list_ref, unit_ref, sem = refs
    per = msgs[0].shape[1] // BLK
    tiles = half * per
    move = pltpu.make_async_copy(lists_ref, list_ref, sem)
    move.start()
    me = me_ref[0]
    for m in range(half):
        stage_block(msgs[m], vecs, (me ^ (2 * m + 1)) * per, right_ref, vec_ref)
    factors = jnp.concatenate([factor_ref[0:1, :]] * GROUP, axis=1)
    move.wait()
    start = 0
    for r in range(tiles):
        for k in range(most):
            unit_ref[start + k] = r * BLK + k * GROUP
        start = start + list_ref[r, BLK - 1]
    for k in range(BIG):
        unit_ref[start + k] = tiles * BLK

    def visit(code):
        r = lax.shift_right_logical(code, 7)
        k = lax.bitwise_and(code, BLK - 1)
        ids = [list_ref[r, k + q] for q in range(GROUP)]
        right = jnp.concatenate([right_ref[b] for b in ids], axis=1)
        arg = lax.dot_general(left_ref[r], right, (((1,), (0,)), ((), ())), preferred_element_type=jnp.float32)
        kernel = jnp.exp2(arg * factors)
        weights = kernel.astype(jnp.bfloat16)
        total = kernel[:, 0:BLK]
        for q in range(1, GROUP):
            total = total + kernel[:, q * BLK : (q + 1) * BLK]
        vec = jnp.concatenate([vec_ref[b] for b in ids], axis=1)
        push = lax.dot_general(vec, weights, (((1,), (1,)), ((), ())), preferred_element_type=jnp.float32)
        sums_ref[r] = sums_ref[r] + total
        pushed_ref[r] = pushed_ref[r] + push

    def big_step(t, carry):
        for g in range(BIG):
            visit(unit_ref[t * BIG + g])
        return carry

    def small_step(t, first):
        for g in range(SMALL):
            visit(unit_ref[first + t * SMALL + g])
        return first

    bigs = lax.div(start + ROUND, BIG)
    rest = jnp.maximum(start - bigs * BIG, 0)
    lax.fori_loop(0, bigs, big_step, 0)
    lax.fori_loop(0, lax.div(rest + (SMALL - 1), SMALL), small_step, bigs * BIG)
    for r in range(tiles):
        row_sum = jnp.sum(sums_ref[r].T, axis=0, keepdims=True)
        scaled_ref[:, r * BLK : (r + 1) * BLK] = (pushed_ref[r] / (row_sum * row_sum)).astype(jnp.bfloat16)


def pull_tile(piece, kernel, colm_ref, c, block):
    parts = []
    for h in range(piece.shape[1] // BLK):
        m = colm_ref[c, block + h : block + h + 1, :]
        part = piece[:, h * BLK : (h + 1) * BLK].astype(jnp.float32)
        parts.append(jnp.where(m > 0.5, part, 0.0).astype(jnp.bfloat16))
    return lax.dot_general(
        jnp.concatenate(parts, axis=1), kernel, (((1,), (1,)), ((), ())), preferred_element_type=jnp.float32
    )


def own_kernel(n, vecs, me_ref, factor_ref, left_ref, scaled_ref, *refs):
    msgs, (partial_ref, kern_ref, colm_ref, rows_ref) = refs[:n], refs[n:]
    rows = msgs[0].shape[1]
    per = rows // BLK
    me = me_ref[0]
    left = jnp.concatenate([left_ref[c] for c in range(per)], axis=0)
    factors = jnp.concatenate([factor_ref[0:1, :]] * per, axis=1)
    for o in range(n):
        links = msgs[o][msgs[o].shape[0] - AUX :, :].astype(jnp.float32)[LINK_ROW : LINK_ROW + 1, :]
        for h in range(per):
            rows_ref[o * per + h : o * per + h + 1, :] = links[:, h * BLK : (h + 1) * BLK]
    table = rows_ref[...]
    lane = lax.broadcasted_iota(jnp.int32, table.shape, 1)
    for c in range(per):
        picked = jnp.sum(jnp.where(lane == me * per + c, table, 0.0), axis=1, keepdims=True)
        colm_ref[c] = jnp.broadcast_to(picked, table.shape)
    total = [jnp.zeros((vecs, BLK), jnp.float32) for _ in range(per)]
    for o in range(n):
        right = right_side(msgs[o], vecs, slice(0, rows))
        arg = lax.dot_general(left, right, (((1,), (0,)), ((), ())), preferred_element_type=jnp.float32)
        weights = jnp.exp2(arg * factors).astype(jnp.bfloat16)
        if o % 2:
            kern_ref[o // 2] = weights
        else:
            piece = scaled_ref[:, o // 2 * rows : (o // 2 + 1) * rows]
            for c in range(per):
                total[c] = total[c] + pull_tile(piece, weights[c * BLK : (c + 1) * BLK, :], colm_ref, c, o * per)
    for c in range(per):
        partial_ref[:, c * BLK : (c + 1) * BLK] = total[c]


def pull_kernel(n, partial_ref, colm_ref, kern_ref, scaled_ref, out_ref):
    rows = out_ref.shape[1]
    per = rows // BLK
    for c in range(per):
        cols = slice(c * BLK, (c + 1) * BLK)
        total = partial_ref[:, cols]
        for m in range(n // 2):
            piece = scaled_ref[:, m * rows : (m + 1) * rows]
            total = total + pull_tile(piece, kern_ref[m, cols, :], colm_ref, c, (2 * m + 1) * per)
        out_ref[:, cols] = total


def in_hbm(*arrays):
    return [pltpu.with_memory_space_constraint(a, pltpu.HBM) for a in arrays]


def add_kernel(a_ref, b_ref, out_ref):
    out_ref[...] = a_ref[...] + b_ref[...]


def per_device(n, slices, states, vectors, kernel_scale, neighbour_blocks, neighbour_count):
    coords, rows = states.shape[1], states.shape[2]
    vecs = vectors.shape[0]
    per = rows // BLK
    depth = 4 * coords + AUX
    me = lax.axis_index("traj").astype(jnp.int32).reshape(1)
    msg = pl.pallas_call(
        functools.partial(prep_kernel, n * per),
        out_shape=jax.ShapeDtypeStruct((vecs + 2 * coords + AUX, rows), jnp.bfloat16),
        in_specs=[HBM] * 4,
        out_specs=VMEM,
        scratch_shapes=[
            pltpu.SMEM(neighbour_blocks.shape, jnp.int32),
            pltpu.SMEM(neighbour_count.shape, jnp.int32),
            pltpu.VMEM(states.shape, jnp.float32),
            pltpu.SemaphoreType.DMA((4,)),
        ],
        compiler_params=PARAMS,
        name="prep",
    )(*in_hbm(neighbour_blocks, neighbour_count, states, vectors))
    factor = pl.pallas_call(
        factor_kernel,
        out_shape=jax.ShapeDtypeStruct((8, BLK), jnp.float32),
        in_specs=[SMEM],
        out_specs=VMEM,
        compiler_params=PARAMS,
        cost_estimate=pl.CostEstimate(flops=COVER, bytes_accessed=1 << 12, transcendentals=0),
        name="factor",
    )(kernel_scale)
    msgs, factor = staged_gather(msg, n, "traj", factor)
    half = n // 2
    tiles = half * per
    most = -(-neighbour_blocks.shape[1] // GROUP)
    shared = (
        jax.ShapeDtypeStruct((n * per + 1, depth, BLK), jnp.bfloat16),
        jax.ShapeDtypeStruct((n * per + 1, vecs, BLK), jnp.bfloat16),
        jax.ShapeDtypeStruct((tiles + 1, BLK, BLK), jnp.float32),
        jax.ShapeDtypeStruct((tiles + 1, vecs, BLK), jnp.float32),
    )
    lefts, lists, *state = pl.pallas_call(
        functools.partial(left_kernel, half, vecs),
        out_shape=(
            jax.ShapeDtypeStruct((tiles + 1, BLK, depth), jnp.bfloat16),
            jax.ShapeDtypeStruct((tiles + 8, BLK), jnp.int32),
            *shared,
        ),
        in_specs=[SMEM] + [VMEM] * half,
        out_specs=(VMEM,) * 6,
        compiler_params=PARAMS,
        name="left",
    )(me, *msgs[::2])
    scaled = pl.pallas_call(
        functools.partial(push_kernel, half, vecs, most),
        out_shape=(*shared, jax.ShapeDtypeStruct((vecs, half * rows), jnp.bfloat16)),
        in_specs=[SMEM] + [VMEM] * (half + 7),
        out_specs=(VMEM,) * 5,
        input_output_aliases={4 + half + i: i for i in range(4)},
        scratch_shapes=[
            pltpu.SMEM((tiles + 8, BLK), jnp.int32),
            pltpu.SMEM((tiles * most + most + BIG,), jnp.int32),
            pltpu.SemaphoreType.DMA,
        ],
        compiler_params=PARAMS,
        name="push",
    )(me, factor, lists, lefts, *msgs[1::2], *state)[4]
    across = lax.ppermute(scaled, "traj", [(i, i ^ 1) for i in range(n)])
    partial, kern, colm = pl.pallas_call(
        functools.partial(own_kernel, n, vecs),
        out_shape=(
            jax.ShapeDtypeStruct((vecs, rows), jnp.float32),
            jax.ShapeDtypeStruct((half, rows, rows), jnp.bfloat16),
            jax.ShapeDtypeStruct((per, n * per, BLK), jnp.float32),
        ),
        in_specs=[SMEM, VMEM, VMEM, VMEM] + [VMEM] * n,
        out_specs=(VMEM, VMEM, VMEM),
        scratch_shapes=[pltpu.VMEM((n * per, BLK), jnp.float32)],
        compiler_params=PARAMS,
        cost_estimate=pl.CostEstimate(flops=2 * n * rows * rows * (depth + vecs), bytes_accessed=1 << 20, transcendentals=0),
        name="own",
    )(me, factor, lefts, scaled, *msgs)
    total = pl.pallas_call(
        functools.partial(pull_kernel, n),
        out_shape=jax.ShapeDtypeStruct((vecs, rows), jnp.float32),
        in_specs=[VMEM] * 4,
        out_specs=VMEM,
        compiler_params=PARAMS,
        name="pull",
    )(partial, colm, kern, across)
    hop = 1
    while hop < slices:
        other = lax.ppermute(total, "tm", [(i, i ^ hop) for i in range(slices)])
        total = pl.pallas_call(
            add_kernel,
            out_shape=jax.ShapeDtypeStruct((vecs, rows), jnp.float32),
            in_specs=[VMEM, VMEM],
            out_specs=VMEM,
            compiler_params=PARAMS,
            name="add",
        )(total, other)
        hop *= 2
    return total


def solution(mesh):
    in_specs = (P("tm", None, "traj"), P(None, "traj"), P("tm"), P("traj", None), P("traj"))
    out_specs = P(None, "traj")
    n = mesh.shape["traj"]

    def body(*args):
        return per_device(n, mesh.shape["tm"], *args)

    return jax.shard_map(body, mesh=mesh, in_specs=in_specs, out_specs=out_specs, check_vma=False)
```

profile of v0, /device:TPU:0, one launch (start us, length us, event | category | flops | bytes accessed | tf_op | source)
XLA Modules:
  0.0 32.8 jit_solution(4313768607745287840)
XLA Ops:
  0.0 0.9 %prep.1.refs_0_ = bf16[136,256]{1,0:T(8,128)(2,1)S(1)} custom-call(s32[2,24]{1,0:T(2,128)} %lists_hbm.1, s32[2]{0:T(128)} %count_hbm.1, f32[1,32,256]{2,1,0:T(8,128)} %states_hbm.1, bf16[64,256]{1,0:T(8,128)(2,1)} %vectors_hbm.1), custom_call_target="tpu_custom_call" | custom-call | tf_op jit(solution)/shard_map/prep/pallas_call | solution.py:273
  0.9 4.1 %collective-permute-start.3 = (bf16[136,256]{1,0:T(8,128)(2,1)S(1)}, bf16[136,256]{1,0:T(8,128)(2,1)S(1)}, u32[]{:S(2)}, u32[]{:S(2)}) collective-permute-start(bf16[136,256]{1,0:T(8,128)(2,1)S(1)} %prep.1.refs_0_), channel_id=1, source_target_pairs={{0,16},{2,18},{4,20},{6,22},{8,24},{10,26},{12,28},{14,30},{16,0},... | collective-permute-start | bytes 208904 | tf_op jit(solution)/shard_map/ppermute | solution.py:55
  5.7 1.6 %collective-permute-start.1 = (bf16[136,256]{1,0:T(8,128)(2,1)S(1)}, bf16[136,256]{1,0:T(8,128)(2,1)S(1)}, u32[]{:S(2)}, u32[]{:S(2)}) collective-permute-start(bf16[136,256]{1,0:T(8,128)(2,1)S(1)} %prep.1.refs_0_), channel_id=1, source_target_pairs={{0,8},{2,10},{4,12},{6,14},{8,0},{10,2},{12,4},{14,6},{16,24},{18,... | collective-permute-start | bytes 208904 | tf_op jit(solution)/shard_map/ppermute | solution.py:55
  7.3 1.5 %collective-permute-start = (bf16[136,256]{1,0:T(8,128)(2,1)S(1)}, bf16[136,256]{1,0:T(8,128)(2,1)S(1)}, u32[]{:S(2)}, u32[]{:S(2)}) collective-permute-start(bf16[136,256]{1,0:T(8,128)(2,1)S(1)} %prep.1.refs_0_), channel_id=1, source_target_pairs={{0,4},{2,6},{4,0},{6,2},{8,12},{10,14},{12,8},{14,10},{16,20},{18,... | collective-permute-start | bytes 208904 | tf_op jit(solution)/shard_map/ppermute | solution.py:55
  8.8 0.0 collective-permute-start.7
  8.8 0.0 collective-permute-done.3.refs_4_.refs_8_
  8.9 0.8 %collective-permute-start.5 = (bf16[136,256]{1,0:T(8,128)(2,1)S(1)}, bf16[136,256]{1,0:T(8,128)(2,1)S(1)}, u32[]{:S(2)}, u32[]{:S(2)}) collective-permute-start(bf16[136,256]{1,0:T(8,128)(2,1)S(1)} %collective-permute-done.3.refs_4_.refs_8_), channel_id=1, source_target_pairs={{0,8},{2,10},{4,12},{6,14},{8,0},{10,2},{12,4},{14,6},{16,24},{18,... | collective-permute-start | bytes 208904 | tf_op jit(solution)/shard_map/ppermute | solution.py:55
  9.7 0.4 %collective-permute-done.1.refs_2_.refs_4_ = bf16[136,256]{1,0:T(8,128)(2,1)S(1)} collective-permute-done((bf16[136,256]{1,0:T(8,128)(2,1)S(1)}, bf16[136,256]{1,0:T(8,128)(2,1)S(1)}, u32[]{:S(2)}, u32[]{:S(2)}) %collective-permute-start.1) | collective-permute-done | bytes 69664 | tf_op jit(solution)/shard_map/ppermute | solution.py:55
  10.1 0.0 collective-permute-start.9
  10.1 1.5 %collective-permute-start.2 = (bf16[136,256]{1,0:T(8,128)(2,1)S(1)}, bf16[136,256]{1,0:T(8,128)(2,1)S(1)}, u32[]{:S(2)}, u32[]{:S(2)}) collective-permute-start(bf16[136,256]{1,0:T(8,128)(2,1)S(1)} %collective-permute-done.1.refs_2_.refs_4_), channel_id=1, source_target_pairs={{0,4},{2,6},{4,0},{6,2},{8,12},{10,14},{12,8},{14,10},{16,20},{18,... | collective-permute-start | bytes 208904 | tf_op jit(solution)/shard_map/ppermute | solution.py:55
  11.6 0.1 collective-permute-done.refs_1_.refs_2_
  11.6 0.2 collective-permute-start.8
  11.8 0.0 collective-permute-done.7.refs_0_.refs_1_
  11.8 1.3 %collective-permute-start.4 = (bf16[136,256]{1,0:T(8,128)(2,1)S(1)}, bf16[136,256]{1,0:T(8,128)(2,1)S(1)}, u32[]{:S(2)}, u32[]{:S(2)}) collective-permute-start(bf16[136,256]{1,0:T(8,128)(2,1)S(1)} %collective-permute-done.3.refs_4_.refs_8_), channel_id=1, source_target_pairs={{0,4},{2,6},{4,0},{6,2},{8,12},{10,14},{12,8},{14,10},{16,20},{18,... | collective-permute-start | bytes 208904 | tf_op jit(solution)/shard_map/ppermute | solution.py:55
  13.2 0.3 collective-permute-done.5.refs_6_.refs_12_
  13.4 1.0 %collective-permute-start.6 = (bf16[136,256]{1,0:T(8,128)(2,1)S(1)}, bf16[136,256]{1,0:T(8,128)(2,1)S(1)}, u32[]{:S(2)}, u32[]{:S(2)}) collective-permute-start(bf16[136,256]{1,0:T(8,128)(2,1)S(1)} %collective-permute-done.5.refs_6_.refs_12_), channel_id=1, source_target_pairs={{0,4},{2,6},{4,0},{6,2},{8,12},{10,14},{12,8},{14,10},{16,20},{18,... | collective-permute-start | bytes 208904 | tf_op jit(solution)/shard_map/ppermute | solution.py:55
  14.5 0.2 collective-permute-done.2.refs_3_.refs_6_
  14.7 0.3 collective-permute-start.13
  15.0 0.2 collective-permute-start.10
  15.2 1.3 %collective-permute-done.4.refs_5_.refs_10_ = bf16[136,256]{1,0:T(8,128)(2,1)S(1)} collective-permute-done((bf16[136,256]{1,0:T(8,128)(2,1)S(1)}, bf16[136,256]{1,0:T(8,128)(2,1)S(1)}, u32[]{:S(2)}, u32[]{:S(2)}) %collective-permute-start.4) | collective-permute-done | bytes 69664 | tf_op jit(solution)/shard_map/ppermute | solution.py:55
  16.5 1.3 %collective-permute-done.6.refs_7_.refs_14_ = bf16[136,256]{1,0:T(8,128)(2,1)S(1)} collective-permute-done((bf16[136,256]{1,0:T(8,128)(2,1)S(1)}, bf16[136,256]{1,0:T(8,128)(2,1)S(1)}, u32[]{:S(2)}, u32[]{:S(2)}) %collective-permute-start.6) | collective-permute-done | bytes 69664 | tf_op jit(solution)/shard_map/ppermute | solution.py:55
  17.8 0.5 %left.1 = (bf16[17,128,136]{2,1,0:T(8,128)(2,1)S(1)}, s32[24,128]{1,0:T(8,128)S(1)}, bf16[33,136,128]{2,1,0:T(8,128)(2,1)S(1)}, bf16[33,64,128]{2,1,0:T(8,128)(2...) custom-call(s32[1]{0:T(128)} %bitcast.me_ref, bf16[136,256]{1,0:T(8,128)(2,1)S(1)} %prep.1.refs_0_, ...), custom_call_target="tpu_custom_call" | custom-call | tf_op jit(solution)/shard_map/left/pallas_call | solution.py:306
  18.3 0.0 collective-permute-done.10.refs_3_.refs_7_
  18.3 0.0 collective-permute-done.13.refs_6_.refs_13_
  18.3 0.7 %collective-permute-done.14.refs_7_.refs_15_ = bf16[136,256]{1,0:T(8,128)(2,1)S(1)} collective-permute-done((bf16[136,256]{1,0:T(8,128)(2,1)S(1)}, bf16[136,256]{1,0:T(8,128)(2,1)S(1)}, u32[]{:S(2)}, u32[]{:S(2)}) %collective-permute-start.14) | collective-permute-done | bytes 69664 | tf_op jit(solution)/shard_map/ppermute | solution.py:55
  19.0 5.7 %push.1 = (bf16[33,136,128]{2,1,0:T(8,128)(2,1)S(1)}, bf16[33,64,128]{2,1,0:T(8,128)(2,1)S(1)}, f32[17,128,128]{2,1,0:T(8,128)S(1)}, f32[17,64,128]{2,1,0:T(8,128)S(1)}, bf16[64,2048]{1,0:T(8,128)(2,1)S(1)}) custom-call(s32[1]{0:T(128)} %bitcast.me_ref, ...), custom_call_target="tpu_custom_call", output_to_operand_aliasing={{0}: (12, {}), {1}: (13, {}), {2}: (14, {}), {3}: (15, {})} | custom-call | tf_op jit(solution)/shard_map/push/pallas_call | solution.py:318
  24.7 0.8 %collective-permute-start.15 = (bf16[64,2048]{1,0:T(8,128)(2,1)S(1)}, bf16[64,2048]{1,0:T(8,128)(2,1)S(1)}, u32[]{:S(2)}, u32[]{:S(2)}) collective-permute-start(bf16[64,2048]{1,0:T(8,128)(2,1)S(1)} %get-tuple-element.25.scaled_ref), channel_id=1, source_target_pairs={{0,2},{2,0},{4,6},{6,4},{8,10},{10,8},{12,14},{14,12},{16,18},{18,... | collective-permute-start | bytes 786440 | tf_op jit(solution)/shard_map/ppermute | solution.py:332
  25.4 1.9 %own.1 = (f32[64,256]{1,0:T(8,128)S(1)}, bf16[8,256,256]{2,1,0:T(8,128)(2,1)S(1)}, f32[2,32,128]{2,1,0:T(8,128)S(1)}) custom-call(s32[1]{0:T(128)} %bitcast.me_ref, f32[8,128]{1,0:T(8,128)S(1)} %factor.1.factor_ref, bf16[17,128,136]{2,1,0:T(8,128)(2,1)S(1)} %get-tuple-element.19.left_ref, bf16[64,2048]{1,0:T(8,128)(2,1)S(1)} %get-tuple-element.25.scaled_ref, ...), custom_call_target="tpu_custom_call" | custom-call | flops 419430400 | bytes 1048576 | tf_op jit(solution)/shard_map/own/pallas_call | solution.py:333
  27.3 0.5 %pull.1.a_ref = f32[64,256]{1,0:T(8,128)S(1)} custom-call(f32[64,256]{1,0:T(8,128)S(1)} %get-tuple-element.26.partial_ref, f32[2,32,128]{2,1,0:T(8,128)S(1)} %get-tuple-element.27.colm_ref, bf16[8,256,256]{2,1,0:T(8,128)(2,1)S(1)} %get-tuple-element.28.kern_ref, bf16[64,2048]{1,0:T(8,128)(2,1)S(1)} %collective-permute-done.15.scaled_ref), custom_call_target="tpu_custom_call" | custom-call | tf_op jit(solution)/shard_map/pull/pallas_call | solution.py:347
  27.8 1.6 %collective-permute-start.16 = (f32[64,256]{1,0:T(8,128)S(1)}, f32[64,256]{1,0:T(8,128)S(1)}, u32[]{:S(2)}, u32[]{:S(2)}) collective-permute-start(f32[64,256]{1,0:T(8,128)S(1)} %pull.1.a_ref), channel_id=1, source_target_pairs={{0,1},{1,0},{2,3},{3,2},{4,5},{5,4},{6,7},{7,6},{8,9},{9,8},{10,11... | collective-permute-start | bytes 196616 | tf_op jit(solution)/shard_map/ppermute | solution.py:357
  29.3 2.8 %collective-permute-done.16.b_ref = f32[64,256]{1,0:T(8,128)S(1)} collective-permute-done((f32[64,256]{1,0:T(8,128)S(1)}, f32[64,256]{1,0:T(8,128)S(1)}, u32[]{:S(2)}, u32[]{:S(2)}) %collective-permute-start.16) | collective-permute-done | bytes 65568 | tf_op jit(solution)/shard_map/ppermute | solution.py:357
  32.1 0.6 %add.1 = f32[64,256]{1,0:T(8,128)} custom-call(f32[64,256]{1,0:T(8,128)S(1)} %pull.1.a_ref, f32[64,256]{1,0:T(8,128)S(1)} %collective-permute-done.16.b_ref), custom_call_target="tpu_custom_call" | custom-call | tf_op jit(solution)/shard_map/add/pallas_call | solution.py:358
  (9 shorter events, 0.0 us)
Async XLA Ops:
  0.9 8.0 %collective-permute-start.3 = (bf16[136,256]{1,0:T(8,128)(2,1)S(1)}, bf16[136,256]{1,0:T(8,128)(2,1)S(1)}, u32[]{:S(2)}, u32[]{:S(2)}) collective-permute-start(bf16[136,256]{1,0:T(8,128)(2,1)S(1)} %prep.1.refs_0_), channel_id=1, source_target_pairs={{0,16},{2,18},{4,20},{6,22},{8,24},{10,26},{12,28},{14,30},{16,0},... | collective-permute-start | bytes 208904 | tf_op jit(solution)/shard_map/ppermute | solution.py:55
  5.7 4.4 %collective-permute-start.1 = (bf16[136,256]{1,0:T(8,128)(2,1)S(1)}, bf16[136,256]{1,0:T(8,128)(2,1)S(1)}, u32[]{:S(2)}, u32[]{:S(2)}) collective-permute-start(bf16[136,256]{1,0:T(8,128)(2,1)S(1)} %prep.1.refs_0_), channel_id=1, source_target_pairs={{0,8},{2,10},{4,12},{6,14},{8,0},{10,2},{12,4},{14,6},{16,24},{18,... | collective-permute-start | bytes 208904 | tf_op jit(solution)/shard_map/ppermute | solution.py:55
  7.3 4.3 %collective-permute-start = (bf16[136,256]{1,0:T(8,128)(2,1)S(1)}, bf16[136,256]{1,0:T(8,128)(2,1)S(1)}, u32[]{:S(2)}, u32[]{:S(2)}) collective-permute-start(bf16[136,256]{1,0:T(8,128)(2,1)S(1)} %prep.1.refs_0_), channel_id=1, source_target_pairs={{0,4},{2,6},{4,0},{6,2},{8,12},{10,14},{12,8},{14,10},{16,20},{18,... | collective-permute-start | bytes 208904 | tf_op jit(solution)/shard_map/ppermute | solution.py:55
  8.8 3.0 %collective-permute-start.7 = (bf16[136,256]{1,0:T(8,128)(2,1)S(1)}, bf16[136,256]{1,0:T(8,128)(2,1)S(1)}, u32[]{:S(2)}, u32[]{:S(2)}) collective-permute-start(bf16[136,256]{1,0:T(8,128)(2,1)S(1)} %prep.1.refs_0_), channel_id=1, source_target_pairs={{0,2},{2,0},{4,6},{6,4},{8,10},{10,8},{12,14},{14,12},{16,18},{18,... | collective-permute-start | bytes 208904 | tf_op jit(solution)/shard_map/ppermute | solution.py:55
  8.9 4.6 %collective-permute-start.5 = (bf16[136,256]{1,0:T(8,128)(2,1)S(1)}, bf16[136,256]{1,0:T(8,128)(2,1)S(1)}, u32[]{:S(2)}, u32[]{:S(2)}) collective-permute-start(bf16[136,256]{1,0:T(8,128)(2,1)S(1)} %collective-permute-done.3.refs_4_.refs_8_), channel_id=1, source_target_pairs={{0,8},{2,10},{4,12},{6,14},{8,0},{10,2},{12,4},{14,6},{16,24},{18,... | collective-permute-start | bytes 208904 | tf_op jit(solution)/shard_map/ppermute | solution.py:55
  10.1 4.4 %collective-permute-start.9 = (bf16[136,256]{1,0:T(8,128)(2,1)S(1)}, bf16[136,256]{1,0:T(8,128)(2,1)S(1)}, u32[]{:S(2)}, u32[]{:S(2)}) collective-permute-start(bf16[136,256]{1,0:T(8,128)(2,1)S(1)} %collective-permute-done.1.refs_2_.refs_4_), channel_id=1, source_target_pairs={{0,2},{2,0},{4,6},{6,4},{8,10},{10,8},{12,14},{14,12},{16,18},{18,... | collective-permute-start | bytes 208904 | tf_op jit(solution)/shard_map/ppermute | solution.py:55
  10.1 4.6 %collective-permute-start.2 = (bf16[136,256]{1,0:T(8,128)(2,1)S(1)}, bf16[136,256]{1,0:T(8,128)(2,1)S(1)}, u32[]{:S(2)}, u32[]{:S(2)}) collective-permute-start(bf16[136,256]{1,0:T(8,128)(2,1)S(1)} %collective-permute-done.1.refs_2_.refs_4_), channel_id=1, source_target_pairs={{0,4},{2,6},{4,0},{6,2},{8,12},{10,14},{12,8},{14,10},{16,20},{18,... | collective-permute-start | bytes 208904 | tf_op jit(solution)/shard_map/ppermute | solution.py:55
  11.6 3.3 %collective-permute-start.8 = (bf16[136,256]{1,0:T(8,128)(2,1)S(1)}, bf16[136,256]{1,0:T(8,128)(2,1)S(1)}, u32[]{:S(2)}, u32[]{:S(2)}) collective-permute-start(bf16[136,256]{1,0:T(8,128)(2,1)S(1)} %collective-permute-done.refs_1_.refs_2_), channel_id=1, source_target_pairs={{0,2},{2,0},{4,6},{6,4},{8,10},{10,8},{12,14},{14,12},{16,18},{18,... | collective-permute-start | bytes 208904 | tf_op jit(solution)/shard_map/ppermute | solution.py:55
  11.8 4.7 %collective-permute-start.4 = (bf16[136,256]{1,0:T(8,128)(2,1)S(1)}, bf16[136,256]{1,0:T(8,128)(2,1)S(1)}, u32[]{:S(2)}, u32[]{:S(2)}) collective-permute-start(bf16[136,256]{1,0:T(8,128)(2,1)S(1)} %collective-permute-done.3.refs_4_.refs_8_), channel_id=1, source_target_pairs={{0,4},{2,6},{4,0},{6,2},{8,12},{10,14},{12,8},{14,10},{16,20},{18,... | collective-permute-start | bytes 208904 | tf_op jit(solution)/shard_map/ppermute | solution.py:55
  13.4 4.3 %collective-permute-start.6 = (bf16[136,256]{1,0:T(8,128)(2,1)S(1)}, bf16[136,256]{1,0:T(8,128)(2,1)S(1)}, u32[]{:S(2)}, u32[]{:S(2)}) collective-permute-start(bf16[136,256]{1,0:T(8,128)(2,1)S(1)} %collective-permute-done.5.refs_6_.refs_12_), channel_id=1, source_target_pairs={{0,4},{2,6},{4,0},{6,2},{8,12},{10,14},{12,8},{14,10},{16,20},{18,... | collective-permute-start | bytes 208904 | tf_op jit(solution)/shard_map/ppermute | solution.py:55
  14.4 3.9 %collective-permute-start.11 = (bf16[136,256]{1,0:T(8,128)(2,1)S(1)}, bf16[136,256]{1,0:T(8,128)(2,1)S(1)}, u32[]{:S(2)}, u32[]{:S(2)}) collective-permute-start(bf16[136,256]{1,0:T(8,128)(2,1)S(1)} %collective-permute-done.3.refs_4_.refs_8_), channel_id=1, source_target_pairs={{0,2},{2,0},{4,6},{6,4},{8,10},{10,8},{12,14},{14,12},{16,18},{18,... | collective-permute-start | bytes 208904 | tf_op jit(solution)/shard_map/ppermute | solution.py:55
  14.7 3.7 %collective-permute-start.13 = (bf16[136,256]{1,0:T(8,128)(2,1)S(1)}, bf16[136,256]{1,0:T(8,128)(2,1)S(1)}, u32[]{:S(2)}, u32[]{:S(2)}) collective-permute-start(bf16[136,256]{1,0:T(8,128)(2,1)S(1)} %collective-permute-done.5.refs_6_.refs_12_), channel_id=1, source_target_pairs={{0,2},{2,0},{4,6},{6,4},{8,10},{10,8},{12,14},{14,12},{16,18},{18,... | collective-permute-start | bytes 208904 | tf_op jit(solution)/shard_map/ppermute | solution.py:55
  15.0 3.3 %collective-permute-start.10 = (bf16[136,256]{1,0:T(8,128)(2,1)S(1)}, bf16[136,256]{1,0:T(8,128)(2,1)S(1)}, u32[]{:S(2)}, u32[]{:S(2)}) collective-permute-start(bf16[136,256]{1,0:T(8,128)(2,1)S(1)} %collective-permute-done.2.refs_3_.refs_6_), channel_id=1, source_target_pairs={{0,2},{2,0},{4,6},{6,4},{8,10},{10,8},{12,14},{14,12},{16,18},{18,... | collective-permute-start | bytes 208904 | tf_op jit(solution)/shard_map/ppermute | solution.py:55
  16.5 1.8 %collective-permute-start.12 = (bf16[136,256]{1,0:T(8,128)(2,1)S(1)}, bf16[136,256]{1,0:T(8,128)(2,1)S(1)}, u32[]{:S(2)}, u32[]{:S(2)}) collective-permute-start(bf16[136,256]{1,0:T(8,128)(2,1)S(1)} %collective-permute-done.4.refs_5_.refs_10_), channel_id=1, source_target_pairs={{0,2},{2,0},{4,6},{6,4},{8,10},{10,8},{12,14},{14,12},{16,18},{18,... | collective-permute-start | bytes 208904 | tf_op jit(solution)/shard_map/ppermute | solution.py:55
  17.8 1.3 %collective-permute-start.14 = (bf16[136,256]{1,0:T(8,128)(2,1)S(1)}, bf16[136,256]{1,0:T(8,128)(2,1)S(1)}, u32[]{:S(2)}, u32[]{:S(2)}) collective-permute-start(bf16[136,256]{1,0:T(8,128)(2,1)S(1)} %collective-permute-done.6.refs_7_.refs_14_), channel_id=1, source_target_pairs={{0,2},{2,0},{4,6},{6,4},{8,10},{10,8},{12,14},{14,12},{16,18},{18,... | collective-permute-start | bytes 208904 | tf_op jit(solution)/shard_map/ppermute | solution.py:55
  24.7 2.6 %collective-permute-start.15 = (bf16[64,2048]{1,0:T(8,128)(2,1)S(1)}, bf16[64,2048]{1,0:T(8,128)(2,1)S(1)}, u32[]{:S(2)}, u32[]{:S(2)}) collective-permute-start(bf16[64,2048]{1,0:T(8,128)(2,1)S(1)} %get-tuple-element.25.scaled_ref), channel_id=1, source_target_pairs={{0,2},{2,0},{4,6},{6,4},{8,10},{10,8},{12,14},{14,12},{16,18},{18,... | collective-permute-start | bytes 786440 | tf_op jit(solution)/shard_map/ppermute | solution.py:332
  27.8 4.3 %collective-permute-start.16 = (f32[64,256]{1,0:T(8,128)S(1)}, f32[64,256]{1,0:T(8,128)S(1)}, u32[]{:S(2)}, u32[]{:S(2)}) collective-permute-start(f32[64,256]{1,0:T(8,128)S(1)} %pull.1.a_ref), channel_id=1, source_target_pairs={{0,1},{1,0},{2,3},{3,2},{4,5},{5,4},{6,7},{7,6},{8,9},{9,8},{10,11... | collective-permute-start | bytes 196616 | tf_op jit(solution)/shard_map/ppermute | solution.py:357
where the time goes:
time: 32.9 us; the launch traced here: 32.8 us
  starting transfers between devices  15 us (46%)
  Pallas kernels  10 us (30%)
  waiting for transfers between devices  6.98 us (21%)
  between operations  0.75 us (2%)
    ppermute x15, starting transfers between devices, staged_gather(): lax.ppermute(pieces[piece], axis, [(d, d ^ hop) for d in range(n)])  12.7 us
    pallas_call x1, Pallas kernels, per_device(): pl.pallas_call(functools.partial(push_kernel, half, vecs, most), out_shap...  5.65 us
    ppermute x15, waiting for transfers between devices, staged_gather(): lax.ppermute(pieces[piece], axis, [(d, d ^ hop) for d in range(n)])  4.2 us
    ppermute x1, waiting for transfers between devices, per_device(): other = lax.ppermute(total, 'tm', [(i, i ^ hop) for i in range(slices)])  2.78 us
    pallas_call x1, Pallas kernels, per_device(): pl.pallas_call(functools.partial(own_kernel, n, vecs), out_shape=(jax.Sha...  1.85 us
    ppermute x1, starting transfers between devices, per_device(): other = lax.ppermute(total, 'tm', [(i, i ^ hop) for i in range(slices)])  1.55 us
    pallas_call x1, Pallas kernels, per_device(): pl.pallas_call(functools.partial(prep_kernel, n * per), out_shape=jax.Sha...  0.88 us
    ppermute x1, starting transfers between devices, per_device(): across = lax.ppermute(scaled, 'traj', [(i, i ^ 1) for i in range(n)])  0.76 us
  transfers between devices with their start and end apart: 17, of which 8 were waited for; matrix products, arithmetic and copies ran while one was open for 0% of the time, Pallas kernels for 7%

commit v1 on v0

--- a/solution.py
+++ b/solution.py
@@ -47,13 +47,11 @@
     return steps
 
 
-def staged_gather(x, n, axis, tied):
+def staged_gather(x, n, axis):
     pieces = {0: x}
-    for i, (piece, hop) in enumerate(plan(n)):
-        if i == 1:
-            pieces[0], tied = lax.optimization_barrier((pieces[0], tied))
+    for piece, hop in plan(n):
         pieces[piece ^ hop] = lax.ppermute(pieces[piece], axis, [(d, d ^ hop) for d in range(n)])
-    return [pieces[o] for o in range(n)], tied
+    return [pieces[o] for o in range(n)]
 
 
 def split3(value):
@@ -293,7 +291,7 @@
         cost_estimate=pl.CostEstimate(flops=COVER, bytes_accessed=1 << 12, transcendentals=0),
         name="factor",
     )(kernel_scale)
-    msgs, factor = staged_gather(msg, n, "traj", factor)
+    msgs = staged_gather(msg, n, "traj")
     half = n // 2
     tiles = half * per
     most = -(-neighbour_blocks.shape[1] // GROUP)

time: 32.9 us -> 33.1 us (level)
  starting transfers between devices: 15 us -> 16.6 us
  waiting for transfers between devices: 6.98 us -> 5.5 us
    ppermute x15, waiting for transfers between devices: 4.2 us -> 2.72 us  [staged_gather(): lax.ppermute(pieces[piece], axis, [(d, d ^ hop) for d in range(n)])]
    ppermute x15, starting transfers between devices: 12.7 us -> 14 us  [staged_gather(): lax.ppermute(pieces[piece], axis, [(d, d ^ hop) for d in range(n)])]
    ppermute x1, starting transfers between devices: 0.76 us -> 1.12 us  [per_device(): across = lax.ppermute(scaled, 'traj', [(i, i ^ 1) for i in range(n)])]
  transfers between devices with their start and end apart: 17 -> 17, of which waited for: 8 -> 5; matrix products, arithmetic and copies ran while one was open for 0% -> 0% of each run, Pallas kernels for 7% -> 7%
where the time goes in v1:
time: 33.1 us; the launch traced here: 32.9 us
  starting transfers between devices  16.6 us (50%)
  Pallas kernels  10 us (30%)
  waiting for transfers between devices  5.5 us (17%)
  between operations  0.76 us (2%)
    ppermute x15, starting transfers between devices, staged_gather(): lax.ppermute(pieces[piece], axis, [(d, d ^ hop) for d in range(n)])  14 us
    pallas_call x1, Pallas kernels, per_device(): pl.pallas_call(functools.partial(push_kernel, half, vecs, most), out_shap...  5.66 us
    ppermute x1, waiting for transfers between devices, per_device(): other = lax.ppermute(total, 'tm', [(i, i ^ hop) for i in range(slices)])  2.78 us
    ppermute x15, waiting for transfers between devices, staged_gather(): lax.ppermute(pieces[piece], axis, [(d, d ^ hop) for d in range(n)])  2.72 us
    pallas_call x1, Pallas kernels, per_device(): pl.pallas_call(functools.partial(own_kernel, n, vecs), out_shape=(jax.Sha...  1.84 us
    ppermute x1, starting transfers between devices, per_device(): other = lax.ppermute(total, 'tm', [(i, i ^ hop) for i in range(slices)])  1.55 us
    ppermute x1, starting transfers between devices, per_device(): across = lax.ppermute(scaled, 'traj', [(i, i ^ 1) for i in range(n)])  1.12 us
    pallas_call x1, Pallas kernels, per_device(): pl.pallas_call(functools.partial(prep_kernel, n * per), out_shape=jax.Sha...  0.88 us
  transfers between devices with their start and end apart: 17, of which 5 were waited for; matrix products, arithmetic and copies ran while one was open for 0% of the time, Pallas kernels for 7%

profile of v1, /device:TPU:0, one launch (start us, length us, event | category | flops | bytes accessed | tf_op | source)
XLA Modules:
  0.0 32.9 jit_solution(18274433786185266145)
XLA Ops:
  0.0 0.9 %prep.1.refs_0_ = bf16[136,256]{1,0:T(8,128)(2,1)S(1)} custom-call(s32[2,24]{1,0:T(2,128)} %lists_hbm.1, s32[2]{0:T(128)} %count_hbm.1, f32[1,32,256]{2,1,0:T(8,128)} %states_hbm.1, bf16[64,256]{1,0:T(8,128)(2,1)} %vectors_hbm.1), custom_call_target="tpu_custom_call" | custom-call | tf_op jit(solution)/shard_map/prep/pallas_call | solution.py:271
  0.9 4.1 %collective-permute-start.3 = (bf16[136,256]{1,0:T(8,128)(2,1)S(1)}, bf16[136,256]{1,0:T(8,128)(2,1)S(1)}, u32[]{:S(2)}, u32[]{:S(2)}) collective-permute-start(bf16[136,256]{1,0:T(8,128)(2,1)S(1)} %prep.1.refs_0_), channel_id=1, source_target_pairs={{0,16},{2,18},{4,20},{6,22},{8,24},{10,26},{12,28},{14,30},{16,0},... | collective-permute-start | bytes 208904 | tf_op jit(solution)/shard_map/ppermute | solution.py:53
  5.0 0.0 collective-permute-start.7
  5.0 1.6 %collective-permute-start.1 = (bf16[136,256]{1,0:T(8,128)(2,1)S(1)}, bf16[136,256]{1,0:T(8,128)(2,1)S(1)}, u32[]{:S(2)}, u32[]{:S(2)}) collective-permute-start(bf16[136,256]{1,0:T(8,128)(2,1)S(1)} %prep.1.refs_0_), channel_id=1, source_target_pairs={{0,8},{2,10},{4,12},{6,14},{8,0},{10,2},{12,4},{14,6},{16,24},{18,... | collective-permute-start | bytes 208904 | tf_op jit(solution)/shard_map/ppermute | solution.py:53
  6.6 1.5 %collective-permute-start = (bf16[136,256]{1,0:T(8,128)(2,1)S(1)}, bf16[136,256]{1,0:T(8,128)(2,1)S(1)}, u32[]{:S(2)}, u32[]{:S(2)}) collective-permute-start(bf16[136,256]{1,0:T(8,128)(2,1)S(1)} %prep.1.refs_0_), channel_id=1, source_target_pairs={{0,4},{2,6},{4,0},{6,2},{8,12},{10,14},{12,8},{14,10},{16,20},{18,... | collective-permute-start | bytes 208904 | tf_op jit(solution)/shard_map/ppermute | solution.py:53
  8.1 0.1 collective-permute-done.3.refs_4_.refs_8_
  8.2 1.6 %collective-permute-start.5 = (bf16[136,256]{1,0:T(8,128)(2,1)S(1)}, bf16[136,256]{1,0:T(8,128)(2,1)S(1)}, u32[]{:S(2)}, u32[]{:S(2)}) collective-permute-start(bf16[136,256]{1,0:T(8,128)(2,1)S(1)} %collective-permute-done.3.refs_4_.refs_8_), channel_id=1, source_target_pairs={{0,8},{2,10},{4,12},{6,14},{8,0},{10,2},{12,4},{14,6},{16,24},{18,... | collective-permute-start | bytes 208904 | tf_op jit(solution)/shard_map/ppermute | solution.py:53
  9.8 1.7 %collective-permute-start.4 = (bf16[136,256]{1,0:T(8,128)(2,1)S(1)}, bf16[136,256]{1,0:T(8,128)(2,1)S(1)}, u32[]{:S(2)}, u32[]{:S(2)}) collective-permute-start(bf16[136,256]{1,0:T(8,128)(2,1)S(1)} %collective-permute-done.3.refs_4_.refs_8_), channel_id=1, source_target_pairs={{0,4},{2,6},{4,0},{6,2},{8,12},{10,14},{12,8},{14,10},{16,20},{18,... | collective-permute-start | bytes 208904 | tf_op jit(solution)/shard_map/ppermute | solution.py:53
  11.5 0.0 collective-permute-done.1.refs_2_.refs_4_
  11.5 0.2 collective-permute-start.9
  11.7 0.0 collective-permute-done.refs_1_.refs_2_
  11.7 0.7 %collective-permute-start.2 = (bf16[136,256]{1,0:T(8,128)(2,1)S(1)}, bf16[136,256]{1,0:T(8,128)(2,1)S(1)}, u32[]{:S(2)}, u32[]{:S(2)}) collective-permute-start(bf16[136,256]{1,0:T(8,128)(2,1)S(1)} %collective-permute-done.1.refs_2_.refs_4_), channel_id=1, source_target_pairs={{0,4},{2,6},{4,0},{6,2},{8,12},{10,14},{12,8},{14,10},{16,20},{18,... | collective-permute-start | bytes 208904 | tf_op jit(solution)/shard_map/ppermute | solution.py:53
  12.4 0.1 collective-permute-done.5.refs_6_.refs_12_
  12.5 1.9 %collective-permute-start.6 = (bf16[136,256]{1,0:T(8,128)(2,1)S(1)}, bf16[136,256]{1,0:T(8,128)(2,1)S(1)}, u32[]{:S(2)}, u32[]{:S(2)}) collective-permute-start(bf16[136,256]{1,0:T(8,128)(2,1)S(1)} %collective-permute-done.5.refs_6_.refs_12_), channel_id=1, source_target_pairs={{0,4},{2,6},{4,0},{6,2},{8,12},{10,14},{12,8},{14,10},{16,20},{18,... | collective-permute-start | bytes 208904 | tf_op jit(solution)/shard_map/ppermute | solution.py:53
  14.4 0.0 collective-permute-done.11.refs_4_.refs_9_
  14.5 0.0 collective-permute-start.8
  14.5 0.0 collective-permute-done.4.refs_5_.refs_10_
  14.5 0.5 %collective-permute-start.13 = (bf16[136,256]{1,0:T(8,128)(2,1)S(1)}, bf16[136,256]{1,0:T(8,128)(2,1)S(1)}, u32[]{:S(2)}, u32[]{:S(2)}) collective-permute-start(bf16[136,256]{1,0:T(8,128)(2,1)S(1)} %collective-permute-done.5.refs_6_.refs_12_), channel_id=1, source_target_pairs={{0,2},{2,0},{4,6},{6,4},{8,10},{10,8},{12,14},{14,12},{16,18},{18,... | collective-permute-start | bytes 208904 | tf_op jit(solution)/shard_map/ppermute | solution.py:53
  15.0 0.0 collective-permute-done.9.refs_2_.refs_5_
  15.0 0.1 collective-permute-start.12
  15.0 1.7 %collective-permute-done.2.refs_3_.refs_6_ = bf16[136,256]{1,0:T(8,128)(2,1)S(1)} collective-permute-done((bf16[136,256]{1,0:T(8,128)(2,1)S(1)}, bf16[136,256]{1,0:T(8,128)(2,1)S(1)}, u32[]{:S(2)}, u32[]{:S(2)}) %collective-permute-start.2) | collective-permute-done | bytes 69664 | tf_op jit(solution)/shard_map/ppermute | solution.py:53
  16.8 0.0 collective-permute-start.10
  16.8 0.8 %collective-permute-done.6.refs_7_.refs_14_ = bf16[136,256]{1,0:T(8,128)(2,1)S(1)} collective-permute-done((bf16[136,256]{1,0:T(8,128)(2,1)S(1)}, bf16[136,256]{1,0:T(8,128)(2,1)S(1)}, u32[]{:S(2)}, u32[]{:S(2)}) %collective-permute-start.6) | collective-permute-done | bytes 69664 | tf_op jit(solution)/shard_map/ppermute | solution.py:53
  18.2 0.5 %left.1 = (bf16[17,128,136]{2,1,0:T(8,128)(2,1)S(1)}, s32[24,128]{1,0:T(8,128)S(1)}, bf16[33,136,128]{2,1,0:T(8,128)(2,1)S(1)}, bf16[33,64,128]{2,1,0:T(8,128)(2...) custom-call(s32[1]{0:T(128)} %bitcast.me_ref, bf16[136,256]{1,0:T(8,128)(2,1)S(1)} %prep.1.refs_0_, ...), custom_call_target="tpu_custom_call" | custom-call | tf_op jit(solution)/shard_map/left/pallas_call | solution.py:304
  18.8 0.0 collective-permute-done.14.refs_7_.refs_15_
  18.8 5.7 %push.1 = (bf16[33,136,128]{2,1,0:T(8,128)(2,1)S(1)}, bf16[33,64,128]{2,1,0:T(8,128)(2,1)S(1)}, f32[17,128,128]{2,1,0:T(8,128)S(1)}, f32[17,64,128]{2,1,0:T(8,128)S(1)}, bf16[64,2048]{1,0:T(8,128)(2,1)S(1)}) custom-call(s32[1]{0:T(128)} %bitcast.me_ref, ...), custom_call_target="tpu_custom_call", output_to_operand_aliasing={{0}: (12, {}), {1}: (13, {}), {2}: (14, {}), {3}: (15, {})} | custom-call | tf_op jit(solution)/shard_map/push/pallas_call | solution.py:316
  24.5 1.1 %collective-permute-start.15 = (bf16[64,2048]{1,0:T(8,128)(2,1)S(1)}, bf16[64,2048]{1,0:T(8,128)(2,1)S(1)}, u32[]{:S(2)}, u32[]{:S(2)}) collective-permute-start(bf16[64,2048]{1,0:T(8,128)(2,1)S(1)} %get-tuple-element.21.scaled_ref), channel_id=1, source_target_pairs={{0,2},{2,0},{4,6},{6,4},{8,10},{10,8},{12,14},{14,12},{16,18},{18,... | collective-permute-start | bytes 786440 | tf_op jit(solution)/shard_map/ppermute | solution.py:330
  25.6 1.8 %own.1 = (f32[64,256]{1,0:T(8,128)S(1)}, bf16[8,256,256]{2,1,0:T(8,128)(2,1)S(1)}, f32[2,32,128]{2,1,0:T(8,128)S(1)}) custom-call(s32[1]{0:T(128)} %bitcast.me_ref, f32[8,128]{1,0:T(8,128)S(1)} %factor.1.factor_ref, bf16[17,128,136]{2,1,0:T(8,128)(2,1)S(1)} %get-tuple-element.15.left_ref, bf16[64,2048]{1,0:T(8,128)(2,1)S(1)} %get-tuple-element.21.scaled_ref, ...), custom_call_target="tpu_custom_call" | custom-call | flops 419430400 | bytes 1048576 | tf_op jit(solution)/shard_map/own/pallas_call | solution.py:331
  27.5 0.5 %pull.1.a_ref = f32[64,256]{1,0:T(8,128)S(1)} custom-call(f32[64,256]{1,0:T(8,128)S(1)} %get-tuple-element.22.partial_ref, f32[2,32,128]{2,1,0:T(8,128)S(1)} %get-tuple-element.23.colm_ref, bf16[8,256,256]{2,1,0:T(8,128)(2,1)S(1)} %get-tuple-element.24.kern_ref, bf16[64,2048]{1,0:T(8,128)(2,1)S(1)} %collective-permute-done.15.scaled_ref), custom_call_target="tpu_custom_call" | custom-call | tf_op jit(solution)/shard_map/pull/pallas_call | solution.py:345
  28.0 1.6 %collective-permute-start.16 = (f32[64,256]{1,0:T(8,128)S(1)}, f32[64,256]{1,0:T(8,128)S(1)}, u32[]{:S(2)}, u32[]{:S(2)}) collective-permute-start(f32[64,256]{1,0:T(8,128)S(1)} %pull.1.a_ref), channel_id=1, source_target_pairs={{0,1},{1,0},{2,3},{3,2},{4,5},{5,4},{6,7},{7,6},{8,9},{9,8},{10,11... | collective-permute-start | bytes 196616 | tf_op jit(solution)/shard_map/ppermute | solution.py:355
  29.5 2.8 %collective-permute-done.16.b_ref = f32[64,256]{1,0:T(8,128)S(1)} collective-permute-done((f32[64,256]{1,0:T(8,128)S(1)}, f32[64,256]{1,0:T(8,128)S(1)}, u32[]{:S(2)}, u32[]{:S(2)}) %collective-permute-start.16) | collective-permute-done | bytes 65568 | tf_op jit(solution)/shard_map/ppermute | solution.py:355
  32.3 0.6 %add.1 = f32[64,256]{1,0:T(8,128)} custom-call(f32[64,256]{1,0:T(8,128)S(1)} %pull.1.a_ref, f32[64,256]{1,0:T(8,128)S(1)} %collective-permute-done.16.b_ref), custom_call_target="tpu_custom_call" | custom-call | tf_op jit(solution)/shard_map/add/pallas_call | solution.py:356
  (9 shorter events, 0.0 us)
Async XLA Ops:
  0.9 7.3 %collective-permute-start.3 = (bf16[136,256]{1,0:T(8,128)(2,1)S(1)}, bf16[136,256]{1,0:T(8,128)(2,1)S(1)}, u32[]{:S(2)}, u32[]{:S(2)}) collective-permute-start(bf16[136,256]{1,0:T(8,128)(2,1)S(1)} %prep.1.refs_0_), channel_id=1, source_target_pairs={{0,16},{2,18},{4,20},{6,22},{8,24},{10,26},{12,28},{14,30},{16,0},... | collective-permute-start | bytes 208904 | tf_op jit(solution)/shard_map/ppermute | solution.py:53
  5.0 4.8 %collective-permute-start.7 = (bf16[136,256]{1,0:T(8,128)(2,1)S(1)}, bf16[136,256]{1,0:T(8,128)(2,1)S(1)}, u32[]{:S(2)}, u32[]{:S(2)}) collective-permute-start(bf16[136,256]{1,0:T(8,128)(2,1)S(1)} %prep.1.refs_0_), channel_id=1, source_target_pairs={{0,2},{2,0},{4,6},{6,4},{8,10},{10,8},{12,14},{14,12},{16,18},{18,... | collective-permute-start | bytes 208904 | tf_op jit(solution)/shard_map/ppermute | solution.py:53
  5.0 6.5 %collective-permute-start.1 = (bf16[136,256]{1,0:T(8,128)(2,1)S(1)}, bf16[136,256]{1,0:T(8,128)(2,1)S(1)}, u32[]{:S(2)}, u32[]{:S(2)}) collective-permute-start(bf16[136,256]{1,0:T(8,128)(2,1)S(1)} %prep.1.refs_0_), channel_id=1, source_target_pairs={{0,8},{2,10},{4,12},{6,14},{8,0},{10,2},{12,4},{14,6},{16,24},{18,... | collective-permute-start | bytes 208904 | tf_op jit(solution)/shard_map/ppermute | solution.py:53
  6.6 5.1 %collective-permute-start = (bf16[136,256]{1,0:T(8,128)(2,1)S(1)}, bf16[136,256]{1,0:T(8,128)(2,1)S(1)}, u32[]{:S(2)}, u32[]{:S(2)}) collective-permute-start(bf16[136,256]{1,0:T(8,128)(2,1)S(1)} %prep.1.refs_0_), channel_id=1, source_target_pairs={{0,4},{2,6},{4,0},{6,2},{8,12},{10,14},{12,8},{14,10},{16,20},{18,... | collective-permute-start | bytes 208904 | tf_op jit(solution)/shard_map/ppermute | solution.py:53
  8.2 4.3 %collective-permute-start.5 = (bf16[136,256]{1,0:T(8,128)(2,1)S(1)}, bf16[136,256]{1,0:T(8,128)(2,1)S(1)}, u32[]{:S(2)}, u32[]{:S(2)}) collective-permute-start(bf16[136,256]{1,0:T(8,128)(2,1)S(1)} %collective-permute-done.3.refs_4_.refs_8_), channel_id=1, source_target_pairs={{0,8},{2,10},{4,12},{6,14},{8,0},{10,2},{12,4},{14,6},{16,24},{18,... | collective-permute-start | bytes 208904 | tf_op jit(solution)/shard_map/ppermute | solution.py:53
  9.8 4.7 %collective-permute-start.11 = (bf16[136,256]{1,0:T(8,128)(2,1)S(1)}, bf16[136,256]{1,0:T(8,128)(2,1)S(1)}, u32[]{:S(2)}, u32[]{:S(2)}) collective-permute-start(bf16[136,256]{1,0:T(8,128)(2,1)S(1)} %collective-permute-done.3.refs_4_.refs_8_), channel_id=1, source_target_pairs={{0,2},{2,0},{4,6},{6,4},{8,10},{10,8},{12,14},{14,12},{16,18},{18,... | collective-permute-start | bytes 208904 | tf_op jit(solution)/shard_map/ppermute | solution.py:53
  9.8 4.7 %collective-permute-start.4 = (bf16[136,256]{1,0:T(8,128)(2,1)S(1)}, bf16[136,256]{1,0:T(8,128)(2,1)S(1)}, u32[]{:S(2)}, u32[]{:S(2)}) collective-permute-start(bf16[136,256]{1,0:T(8,128)(2,1)S(1)} %collective-permute-done.3.refs_4_.refs_8_), channel_id=1, source_target_pairs={{0,4},{2,6},{4,0},{6,2},{8,12},{10,14},{12,8},{14,10},{16,20},{18,... | collective-permute-start | bytes 208904 | tf_op jit(solution)/shard_map/ppermute | solution.py:53
  11.5 3.5 %collective-permute-start.9 = (bf16[136,256]{1,0:T(8,128)(2,1)S(1)}, bf16[136,256]{1,0:T(8,128)(2,1)S(1)}, u32[]{:S(2)}, u32[]{:S(2)}) collective-permute-start(bf16[136,256]{1,0:T(8,128)(2,1)S(1)} %collective-permute-done.1.refs_2_.refs_4_), channel_id=1, source_target_pairs={{0,2},{2,0},{4,6},{6,4},{8,10},{10,8},{12,14},{14,12},{16,18},{18,... | collective-permute-start | bytes 208904 | tf_op jit(solution)/shard_map/ppermute | solution.py:53
  11.7 5.1 %collective-permute-start.2 = (bf16[136,256]{1,0:T(8,128)(2,1)S(1)}, bf16[136,256]{1,0:T(8,128)(2,1)S(1)}, u32[]{:S(2)}, u32[]{:S(2)}) collective-permute-start(bf16[136,256]{1,0:T(8,128)(2,1)S(1)} %collective-permute-done.1.refs_2_.refs_4_), channel_id=1, source_target_pairs={{0,4},{2,6},{4,0},{6,2},{8,12},{10,14},{12,8},{14,10},{16,20},{18,... | collective-permute-start | bytes 208904 | tf_op jit(solution)/shard_map/ppermute | solution.py:53
  12.5 5.1 %collective-permute-start.6 = (bf16[136,256]{1,0:T(8,128)(2,1)S(1)}, bf16[136,256]{1,0:T(8,128)(2,1)S(1)}, u32[]{:S(2)}, u32[]{:S(2)}) collective-permute-start(bf16[136,256]{1,0:T(8,128)(2,1)S(1)} %collective-permute-done.5.refs_6_.refs_12_), channel_id=1, source_target_pairs={{0,4},{2,6},{4,0},{6,2},{8,12},{10,14},{12,8},{14,10},{16,20},{18,... | collective-permute-start | bytes 208904 | tf_op jit(solution)/shard_map/ppermute | solution.py:53
  14.5 4.3 %collective-permute-start.8 = (bf16[136,256]{1,0:T(8,128)(2,1)S(1)}, bf16[136,256]{1,0:T(8,128)(2,1)S(1)}, u32[]{:S(2)}, u32[]{:S(2)}) collective-permute-start(bf16[136,256]{1,0:T(8,128)(2,1)S(1)} %collective-permute-done.refs_1_.refs_2_), channel_id=1, source_target_pairs={{0,2},{2,0},{4,6},{6,4},{8,10},{10,8},{12,14},{14,12},{16,18},{18,... | collective-permute-start | bytes 208904 | tf_op jit(solution)/shard_map/ppermute | solution.py:53
  14.5 4.3 %collective-permute-start.13 = (bf16[136,256]{1,0:T(8,128)(2,1)S(1)}, bf16[136,256]{1,0:T(8,128)(2,1)S(1)}, u32[]{:S(2)}, u32[]{:S(2)}) collective-permute-start(bf16[136,256]{1,0:T(8,128)(2,1)S(1)} %collective-permute-done.5.refs_6_.refs_12_), channel_id=1, source_target_pairs={{0,2},{2,0},{4,6},{6,4},{8,10},{10,8},{12,14},{14,12},{16,18},{18,... | collective-permute-start | bytes 208904 | tf_op jit(solution)/shard_map/ppermute | solution.py:53
  15.0 3.8 %collective-permute-start.12 = (bf16[136,256]{1,0:T(8,128)(2,1)S(1)}, bf16[136,256]{1,0:T(8,128)(2,1)S(1)}, u32[]{:S(2)}, u32[]{:S(2)}) collective-permute-start(bf16[136,256]{1,0:T(8,128)(2,1)S(1)} %collective-permute-done.4.refs_5_.refs_10_), channel_id=1, source_target_pairs={{0,2},{2,0},{4,6},{6,4},{8,10},{10,8},{12,14},{14,12},{16,18},{18,... | collective-permute-start | bytes 208904 | tf_op jit(solution)/shard_map/ppermute | solution.py:53
  16.8 2.1 %collective-permute-start.10 = (bf16[136,256]{1,0:T(8,128)(2,1)S(1)}, bf16[136,256]{1,0:T(8,128)(2,1)S(1)}, u32[]{:S(2)}, u32[]{:S(2)}) collective-permute-start(bf16[136,256]{1,0:T(8,128)(2,1)S(1)} %collective-permute-done.2.refs_3_.refs_6_), channel_id=1, source_target_pairs={{0,2},{2,0},{4,6},{6,4},{8,10},{10,8},{12,14},{14,12},{16,18},{18,... | collective-permute-start | bytes 208904 | tf_op jit(solution)/shard_map/ppermute | solution.py:53
  17.6 1.3 %collective-permute-start.14 = (bf16[136,256]{1,0:T(8,128)(2,1)S(1)}, bf16[136,256]{1,0:T(8,128)(2,1)S(1)}, u32[]{:S(2)}, u32[]{:S(2)}) collective-permute-start(bf16[136,256]{1,0:T(8,128)(2,1)S(1)} %collective-permute-done.6.refs_7_.refs_14_), channel_id=1, source_target_pairs={{0,2},{2,0},{4,6},{6,4},{8,10},{10,8},{12,14},{14,12},{16,18},{18,... | collective-permute-start | bytes 208904 | tf_op jit(solution)/shard_map/ppermute | solution.py:53
  24.5 3.0 %collective-permute-start.15 = (bf16[64,2048]{1,0:T(8,128)(2,1)S(1)}, bf16[64,2048]{1,0:T(8,128)(2,1)S(1)}, u32[]{:S(2)}, u32[]{:S(2)}) collective-permute-start(bf16[64,2048]{1,0:T(8,128)(2,1)S(1)} %get-tuple-element.21.scaled_ref), channel_id=1, source_target_pairs={{0,2},{2,0},{4,6},{6,4},{8,10},{10,8},{12,14},{14,12},{16,18},{18,... | collective-permute-start | bytes 786440 | tf_op jit(solution)/shard_map/ppermute | solution.py:330
  28.0 4.3 %collective-permute-start.16 = (f32[64,256]{1,0:T(8,128)S(1)}, f32[64,256]{1,0:T(8,128)S(1)}, u32[]{:S(2)}, u32[]{:S(2)}) collective-permute-start(f32[64,256]{1,0:T(8,128)S(1)} %pull.1.a_ref), channel_id=1, source_target_pairs={{0,1},{1,0},{2,3},{3,2},{4,5},{5,4},{6,7},{7,6},{8,9},{9,8},{10,11... | collective-permute-start | bytes 196616 | tf_op jit(solution)/shard_map/ppermute | solution.py:355
